TPU v7x, 512 devices: a whole 4x8x8 slice. The times are simulated.
512 devices in a mesh: section: 8 (over y_lo, core), dp: 64 (over y_hi, x, z).
Axes of the slice: x: 4, y: 8 (y_hi: 2, y_lo: 4; y = y_hi * 4 + y_lo), z: 8, core: 2. Of those that a mesh axis runs over, the one named last changes fastest.
Arguments:
- tokens: int32 [8, 5120], P(None, 'dp'), may hold values from 0 to 255
- doc_patches: int32 [8], replicated, may hold values from 160 to 640, as said below
- global_embed: bfloat16 [8, 640, 4096], P('section', 'dp'), may hold values from -6 to 6
- byte_table: bfloat16 [256, 1024], replicated, may hold values from -6 to 6
- w_qkv: bfloat16 [8, 1024, 3072], P('section', 'dp'), may hold values from -0.1875 to 0.1875
- w_out: bfloat16 [8, 1024, 1024], P('section', 'dp'), may hold values from -0.1875 to 0.1875
- layer_gain: bfloat16 [8, 1024], P('section'), may hold values from 0.099609375 to 1.8984375
- w_global: bfloat16 [512, 1024], P(None, 'dp'), may hold values from -0.25 to 0.25
- final_gain: bfloat16 [1024], replicated, may hold values from 0.099609375 to 1.8984375
- w_head: bfloat16 [256, 1024], P(None, 'dp'), may hold values from -0.59765625 to 0.59765625
Outputs:
- logits: bfloat16 [8, 5120, 256], P('section', 'dp')
Inputs may be any that keep to these rules, and one draw needn't show every extreme that they name: Patches from index doc_patches[m] on are padding of micro-batch m; the micro-batches' counts differ from one another.
All inputs are finite; a program needn't handle non-finite values.
Results may differ from a plain program's by a relative error of at most 0.014.
Values may be sent and summed in bfloat16 or wider, within the bound.
No kernel may reach another device: no remote copies, remote signals or barrier semaphores. Data moves between devices by JAX's collectives and lax.ppermute only.
A program may use at most 64 MiB of HBM per device.

v0:
```python
import jax
import jax.numpy as jnp
from jax import lax
from jax.sharding import PartitionSpec as P

HEADS = 16
PATCH = 8


def gather_turned(arrays, axis, dims):
    turned = [jnp.moveaxis(a, dim, 0) for a, dim in zip(arrays, dims)]
    both = jnp.concatenate([t.reshape(len(t), -1) for t in turned], axis=1)
    filled, at, gathered = (lax.all_gather(both, axis, axis=0, tiled=True), 0, [])
    for t, dim in zip(turned, dims):
        piece = filled[:, at : at + t[0].size].reshape(-1, *t.shape[1:])
        gathered.append(jnp.moveaxis(piece, 0, dim))
        at += t[0].size
    return tuple(gathered)


def copy_for_each(shard, axis):
    copies = jnp.broadcast_to(shard, (lax.axis_size(axis), *shard.shape))
    return lax.all_to_all(copies, axis, split_axis=0, concat_axis=0, tiled=True)


def joined_along(pieces, dim):
    lengths = list(pieces.shape[1:])
    lengths[dim] *= pieces.shape[0]
    return jnp.moveaxis(pieces, 0, dim).reshape(lengths)


def gathered_copies(shard, axis, dim):
    pieces = copy_for_each(shard, axis)
    return joined_along(pieces, dim)


def from_behind(block, axis, distance):
    devices = range(lax.axis_size(axis))
    route = [(i - distance, i) for i in devices if i - distance in devices]
    return lax.ppermute(block, axis, route)


def broadcast(shard, axis, root):
    return lax.dynamic_index_in_dim(lax.all_gather(shard, axis), root, 0, keepdims=False)


def norm_rows(hidden, norm_gain):
    scale = lax.rsqrt(jnp.mean(hidden * hidden, axis=-1, keepdims=True) + 1e-06)
    return (hidden * scale * norm_gain.astype(jnp.float32)).astype(jnp.bfloat16)


def attend_layer(inputs, global_add, norm_gain, qkv_weight, out_weight):
    hidden = inputs.astype(jnp.float32) + global_add.astype(jnp.float32)
    normed = norm_rows(hidden, norm_gain)
    projected = jnp.dot(normed, qkv_weight, preferred_element_type=jnp.float32).astype(jnp.bfloat16)
    model_width = inputs.shape[1]
    head_dim = model_width // HEADS
    patch_count = inputs.shape[0] // PATCH

    def split_heads(block):
        return block.reshape(patch_count, PATCH, HEADS, head_dim)

    queries = split_heads(projected[:, :model_width])
    key_rows = split_heads(projected[:, model_width : 2 * model_width])
    value_rows = split_heads(projected[:, 2 * model_width :])
    scores = jnp.einsum(
        "pqhd,pkhd->phqk", queries, key_rows, preferred_element_type=jnp.float32
    ) * head_dim ** (-0.5)
    causal = jnp.tril(jnp.ones((PATCH, PATCH), dtype=jnp.bool_))
    scores = jnp.where(causal, scores, -1e30)
    weights = jax.nn.softmax(scores, axis=-1).astype(jnp.bfloat16)
    context = jnp.einsum("phqk,pkhd->pqhd", weights, value_rows, preferred_element_type=jnp.float32)
    context = context.astype(jnp.bfloat16).reshape(inputs.shape[0], model_width)
    return (hidden + jnp.dot(context, out_weight, preferred_element_type=jnp.float32)).astype(
        jnp.bfloat16
    )


def previous_bytes(byte_ids):
    blocks = byte_ids.reshape(-1, PATCH)
    shifted = jnp.concatenate([jnp.zeros((blocks.shape[0], 1), jnp.int32), blocks[:, :-1]], axis=1)
    return shifted.reshape(-1)


def shards(
    tokens,
    doc_patches,
    global_embed,
    byte_table,
    w_qkv,
    w_out,
    layer_gain,
    w_global,
    final_gain,
    w_head,
):
    sections = lax.axis_size("section")
    section_index = lax.axis_index("section")
    column_index = lax.axis_index("dp")
    micro_count, row_count = tokens.shape
    held_micro = global_embed.shape[0]
    model_width = byte_table.shape[1]
    qkv_full, out_full, global_full, head_full = gather_turned(
        (w_qkv, w_out, w_global, w_head), "dp", (1, 1, 1, 1)
    )
    qkv_full = qkv_full[0]
    out_full = out_full[0]
    norm_gain = layer_gain[0]
    byte_ids = previous_bytes(tokens.reshape(-1))
    one_hot = (
        byte_ids[:, None] == jnp.arange(byte_table.shape[0], dtype=jnp.int32)[None, :]
    ).astype(jnp.bfloat16)
    embeds = jnp.dot(one_hot, byte_table, preferred_element_type=jnp.float32).astype(jnp.bfloat16)
    embeds = embeds.reshape(micro_count, row_count, model_width)
    gathered = gathered_copies(global_embed, "section", 0)
    global_add = jnp.dot(
        gathered.reshape(micro_count * row_count, -1),
        global_full,
        preferred_element_type=jnp.float32,
    )
    global_add = global_add.astype(jnp.bfloat16).reshape(micro_count, row_count, model_width)

    def advance(moment, state):
        incoming, finals = state
        micro_index = moment - section_index
        active = (micro_index >= 0) & (micro_index < micro_count)
        picked = jnp.clip(micro_index, 0, micro_count - 1)
        fresh = lax.dynamic_index_in_dim(embeds, picked, 0, keepdims=False)
        inputs = jnp.where(section_index == 0, fresh, incoming)
        added = lax.dynamic_index_in_dim(global_add, picked, 0, keepdims=False)
        result = lax.cond(
            active,
            lambda: attend_layer(inputs, added, norm_gain, qkv_full, out_full),
            lambda: jnp.zeros_like(inputs),
        )
        previous = lax.dynamic_index_in_dim(finals, picked, 0, keepdims=False)
        keeping = active & (section_index == sections - 1)
        finals = lax.dynamic_update_index_in_dim(
            finals, jnp.where(keeping, result, previous), picked, 0
        )
        incoming = from_behind(result, "section", 1)
        return (incoming, finals)

    initial = (
        jnp.zeros((row_count, model_width), jnp.bfloat16),
        jnp.zeros((micro_count, row_count, model_width), jnp.bfloat16),
    )
    incoming, finals = lax.fori_loop(0, micro_count + sections - 1, advance, initial)
    final_rows = norm_rows(finals.reshape(-1, model_width).astype(jnp.float32), final_gain)
    scores = jnp.einsum("rd,vd->rv", final_rows, head_full, preferred_element_type=jnp.float32)
    scores = scores.reshape(micro_count, row_count, -1)
    patch_start = column_index * (row_count // PATCH)
    patch_of_row = patch_start + jnp.arange(row_count, dtype=jnp.int32) // PATCH
    live_rows = patch_of_row[None, :] < doc_patches[:, None]
    masked = jnp.where(live_rows[:, :, None], scores, 0.0).astype(jnp.bfloat16)
    everyone = broadcast(masked, "section", sections - 1)
    return lax.dynamic_slice_in_dim(everyone, section_index * held_micro, held_micro, 0)


def solution(mesh):
    in_specs = (
        P(None, "dp"),
        P(),
        P("section", "dp", None),
        P(),
        P("section", "dp", None),
        P("section", "dp", None),
        P("section", None),
        P(None, "dp"),
        P(),
        P(None, "dp"),
    )
    out_specs = P("section", "dp", None)
    return jax.shard_map(shards, mesh=mesh, in_specs=in_specs, out_specs=out_specs, check_vma=False)
```

profile of v0, /device:TPU:57, one launch (start us, length us, event | category | flops | bytes accessed | tf_op | source)
XLA Modules:
  0.0 610.4 jit_solution(12505963879059511700)
XLA Ops:
  6.6 1.7 pad_maximum_fusion
  8.3 2.0 broadcast_in_dim.54
  10.3 6.7 %all-to-all-start = ((bf16[8,1,10,4096]{3,2,1,0:T(8,128)(2,1)}), bf16[8,1,10,4096]{3,2,1,0:T(8,128)(2,1)S(1)}, u32[]{:S(2)}, u32[]{:S(2)}) async-start(bf16[8,1,10,4096]{3,2,1,0:T(8,128)(2,1)} %broadcast_in_dim.54), calls=%async_computation | async-start | bytes 2097152 | tf_op jit(solution)/shard_map/all_to_all | solution.py:23
  19.0 24.2 %all-to-all-done = bf16[8,1,10,4096]{3,2,1,0:T(8,128)(2,1)S(1)} async-done(((bf16[8,1,10,4096]{3,2,1,0:T(8,128)(2,1)}), bf16[8,1,10,4096]{3,2,1,0:T(8,128)(2,1)S(1)}, u32[]{:S(2)}, u32[]{:S(2)}) %all-to-all-start) | async-done | bytes 655392 | tf_op jit(solution)/shard_map/all_to_all | solution.py:23
  43.7 165.9 %all-gather.4.cloned.1.call-done = bf16[1024,4864]{1,0:T(8,128)(2,1)} async-done(((bf16[16,4864]{1,0:T(8,128)(2,1)}), bf16[1024,4864]{1,0:T(8,128)(2,1)}) %all-gather.4.cloned.1.call-update) | async-done | bytes 9961488 | tf_op jit(solution)/shard_map/all_gather | solution.py:13
  209.6 5.9 slice.42
  215.5 1.8 slice.43
  217.3 3.2 convolution_convert_fusion.2
  221.7 325.8 %while.16 = (s32[]{:T(128)}, bf16[80,1024]{1,0:T(8,128)(2,1)S(1)}, bf16[8,80,1024]{2,1,0:T(8,128)(2,1)}, s32[]{:T(128)}, pred[]{:T(512)}, /*index=5*/bf16[8,80,1...) while((s32[]{:T(128)}, bf16[80,1024]{1,0:T(8,128)(2,1)S(1)}, ...), condition=%wide.region_6.7_spmd, body=%wide.region_0.6_spmd.sunk | while | flops 676917632 | bytes 15702796 | solution.py:148
  225.4 2.0 collective-permute-done
  231.0 10.1 %collective-permute-done = bf16[80,1024]{1,0:T(8,128)(2,1)S(1)} collective-permute-done((bf16[80,1024]{1,0:T(8,128)(2,1)}, bf16[80,1024]{1,0:T(8,128)(2,1)S(1)}, u32[]{:S(2)}, u32[]{:S(2)}) %collective-permute-start) | collective-permute-done | bytes 163872 | tf_op jit(solution)/shard_map/while/body/eval_jaxpr/ppermute | solution.py:40
  244.7 3.9 collective-permute-done
  252.3 3.9 collective-permute-done
  259.8 3.9 collective-permute-done
  267.3 3.9 collective-permute-done
  274.8 89.9 %collective-permute-done = bf16[80,1024]{1,0:T(8,128)(2,1)S(1)} collective-permute-done((bf16[80,1024]{1,0:T(8,128)(2,1)}, bf16[80,1024]{1,0:T(8,128)(2,1)S(1)}, u32[]{:S(2)}, u32[]{:S(2)}) %collective-permute-start) | collective-permute-done | bytes 163872 | tf_op jit(solution)/shard_map/while/body/eval_jaxpr/ppermute | solution.py:40
  364.7 16.4 %conditional.2 = (bf16[80,1024]{1,0:T(8,128)(2,1)}) conditional(s32[]{:T(128)} %convert_element_type.127, () %tuple.47, (pred[]{:T(512)}, bf16[8,80,1024]{2,1,0:T(8,128)(2,1)}, s32[]{:T(128)}, bf16[80,1024]{1,0:T(8,128)(2,1)S(1)}, bf16[8,80,1024]{2,1,0:T(8,128)(2,1)}, /*index=5*/bf16[1024]{0:T(1024)(128)(2,1)S(1)}, bf16[1024,3072]{1,0:T(8,128)(2,1)}, ...), branch_computations={%region_1.1_spmd, %region_2.5_spmd} | conditional | flops 676835712 | bytes 14227409 | solution.py:131
  365.9 4.2 convolution_convert_fusion
  375.2 2.5 fusion.4
  379.0 2.1 fusion.5
  383.3 1.6 bitcast_dynamic-update-slice_fusion.2
  385.0 3.0 collective-permute-done
  387.9 16.4 %conditional.2 = (bf16[80,1024]{1,0:T(8,128)(2,1)}) conditional(s32[]{:T(128)} %convert_element_type.127, () %tuple.47, (pred[]{:T(512)}, bf16[8,80,1024]{2,1,0:T(8,128)(2,1)}, s32[]{:T(128)}, bf16[80,1024]{1,0:T(8,128)(2,1)S(1)}, bf16[8,80,1024]{2,1,0:T(8,128)(2,1)}, /*index=5*/bf16[1024]{0:T(1024)(128)(2,1)S(1)}, bf16[1024,3072]{1,0:T(8,128)(2,1)}, ...), branch_computations={%region_1.1_spmd, %region_2.5_spmd} | conditional | flops 676835712 | bytes 14227409 | solution.py:131
  389.1 4.2 convolution_convert_fusion
  398.5 2.5 fusion.4
  402.2 2.1 fusion.5
  408.2 3.0 collective-permute-done
  411.1 16.4 %conditional.2 = (bf16[80,1024]{1,0:T(8,128)(2,1)}) conditional(s32[]{:T(128)} %convert_element_type.127, () %tuple.47, (pred[]{:T(512)}, bf16[8,80,1024]{2,1,0:T(8,128)(2,1)}, s32[]{:T(128)}, bf16[80,1024]{1,0:T(8,128)(2,1)S(1)}, bf16[8,80,1024]{2,1,0:T(8,128)(2,1)}, /*index=5*/bf16[1024]{0:T(1024)(128)(2,1)S(1)}, bf16[1024,3072]{1,0:T(8,128)(2,1)}, ...), branch_computations={%region_1.1_spmd, %region_2.5_spmd} | conditional | flops 676835712 | bytes 14227409 | solution.py:131
  412.3 4.2 convolution_convert_fusion
  421.7 2.5 fusion.4
  425.4 2.1 fusion.5
  429.8 1.6 bitcast_dynamic-update-slice_fusion.2
  431.4 3.0 collective-permute-done
  434.4 16.4 %conditional.2 = (bf16[80,1024]{1,0:T(8,128)(2,1)}) conditional(s32[]{:T(128)} %convert_element_type.127, () %tuple.47, (pred[]{:T(512)}, bf16[8,80,1024]{2,1,0:T(8,128)(2,1)}, s32[]{:T(128)}, bf16[80,1024]{1,0:T(8,128)(2,1)S(1)}, bf16[8,80,1024]{2,1,0:T(8,128)(2,1)}, /*index=5*/bf16[1024]{0:T(1024)(128)(2,1)S(1)}, bf16[1024,3072]{1,0:T(8,128)(2,1)}, ...), branch_computations={%region_1.1_spmd, %region_2.5_spmd} | conditional | flops 676835712 | bytes 14227409 | solution.py:131
  435.6 4.2 convolution_convert_fusion
  444.9 2.5 fusion.4
  448.7 2.1 fusion.5
  454.6 3.0 collective-permute-done
  457.6 16.4 %conditional.2 = (bf16[80,1024]{1,0:T(8,128)(2,1)}) conditional(s32[]{:T(128)} %convert_element_type.127, () %tuple.47, (pred[]{:T(512)}, bf16[8,80,1024]{2,1,0:T(8,128)(2,1)}, s32[]{:T(128)}, bf16[80,1024]{1,0:T(8,128)(2,1)S(1)}, bf16[8,80,1024]{2,1,0:T(8,128)(2,1)}, /*index=5*/bf16[1024]{0:T(1024)(128)(2,1)S(1)}, bf16[1024,3072]{1,0:T(8,128)(2,1)}, ...), branch_computations={%region_1.1_spmd, %region_2.5_spmd} | conditional | flops 676835712 | bytes 14227409 | solution.py:131
  458.8 4.2 convolution_convert_fusion
  468.1 2.5 fusion.4
  471.9 2.1 fusion.5
  476.2 1.6 bitcast_dynamic-update-slice_fusion.2
  477.8 3.0 collective-permute-done
  480.8 16.4 %conditional.2 = (bf16[80,1024]{1,0:T(8,128)(2,1)}) conditional(s32[]{:T(128)} %convert_element_type.127, () %tuple.47, (pred[]{:T(512)}, bf16[8,80,1024]{2,1,0:T(8,128)(2,1)}, s32[]{:T(128)}, bf16[80,1024]{1,0:T(8,128)(2,1)S(1)}, bf16[8,80,1024]{2,1,0:T(8,128)(2,1)}, /*index=5*/bf16[1024]{0:T(1024)(128)(2,1)S(1)}, bf16[1024,3072]{1,0:T(8,128)(2,1)}, ...), branch_computations={%region_1.1_spmd, %region_2.5_spmd} | conditional | flops 676835712 | bytes 14227409 | solution.py:131
  482.0 4.2 convolution_convert_fusion
  491.3 2.5 fusion.4
  495.1 2.1 fusion.5
  499.4 1.6 bitcast_dynamic-update-slice_fusion.2
  501.1 3.0 collective-permute-done
  504.0 16.4 %conditional.2 = (bf16[80,1024]{1,0:T(8,128)(2,1)}) conditional(s32[]{:T(128)} %convert_element_type.127, () %tuple.47, (pred[]{:T(512)}, bf16[8,80,1024]{2,1,0:T(8,128)(2,1)}, s32[]{:T(128)}, bf16[80,1024]{1,0:T(8,128)(2,1)S(1)}, bf16[8,80,1024]{2,1,0:T(8,128)(2,1)}, /*index=5*/bf16[1024]{0:T(1024)(128)(2,1)S(1)}, bf16[1024,3072]{1,0:T(8,128)(2,1)}, ...), branch_computations={%region_1.1_spmd, %region_2.5_spmd} | conditional | flops 676835712 | bytes 14227409 | solution.py:131
  505.2 4.2 convolution_convert_fusion
  514.5 2.5 fusion.4
  518.3 2.1 fusion.5
  522.6 1.6 bitcast_dynamic-update-slice_fusion.2
  524.3 3.0 collective-permute-done
  527.2 16.4 %conditional.2 = (bf16[80,1024]{1,0:T(8,128)(2,1)}) conditional(s32[]{:T(128)} %convert_element_type.127, () %tuple.47, (pred[]{:T(512)}, bf16[8,80,1024]{2,1,0:T(8,128)(2,1)}, s32[]{:T(128)}, bf16[80,1024]{1,0:T(8,128)(2,1)S(1)}, bf16[8,80,1024]{2,1,0:T(8,128)(2,1)}, /*index=5*/bf16[1024]{0:T(1024)(128)(2,1)S(1)}, bf16[1024,3072]{1,0:T(8,128)(2,1)}, ...), branch_computations={%region_1.1_spmd, %region_2.5_spmd} | conditional | flops 676835712 | bytes 14227409 | solution.py:131
  528.4 4.2 convolution_convert_fusion
  537.8 2.5 fusion.4
  541.5 2.1 fusion.5
  545.8 1.6 bitcast_dynamic-update-slice_fusion.2
  547.5 1.7 fusion.19
  549.2 2.7 fusion.29
  551.9 50.0 %all-gather.6.cloned.1.call-done = bf16[64,80,256]{2,1,0:T(8,128)(2,1)} async-done(((bf16[8,80,256]{2,1,0:T(8,128)(2,1)}), bf16[64,80,256]{2,1,0:T(8,128)(2,1)}) %all-gather.6.cloned.1.call-update) | async-done | bytes 2621456 | tf_op jit(solution)/shard_map/all_gather | solution.py:44
  (178 shorter events, 117.0 us)
Async XLA Ops:
  6.5 10.9 %copy-start = (bf16[256,1024]{1,0:T(8,128)(2,1)S(1)}, bf16[256,1024]{1,0:T(8,128)(2,1)}, u32[]{:S(2)}) copy-start(bf16[256,1024]{1,0:T(8,128)(2,1)} %param.17) | copy-start | bytes 1572868
  6.5 10.5 %copy-start.2 = (s32[8,80]{1,0:T(8,128)S(1)}, s32[8,80]{1,0:T(8,128)}, u32[]{:S(2)}) copy-start(s32[8,80]{1,0:T(8,128)} %param.14) | copy-start | bytes 7684
  6.5 10.8 %copy-start.3 = (bf16[1024]{0:T(1024)(128)(2,1)S(1)}, bf16[1024]{0:T(1024)(128)(2,1)}, u32[]{:S(2)}) copy-start(bf16[1024]{0:T(1024)(128)(2,1)} %param.22) | copy-start | bytes 6148
  6.5 10.8 %copy-start.1 = (bf16[1,1024]{1,0:T(2,128)(2,1)S(1)}, bf16[1,1024]{1,0:T(2,128)(2,1)}, u32[]{:S(2)}) copy-start(bf16[1,1024]{1,0:T(2,128)(2,1)} %param.20) | copy-start | bytes 6148
  6.5 10.8 %copy-start.4 = (s32[8]{0:T(128)S(1)}, s32[8]{0:T(128)}, u32[]{:S(2)}) copy-start(s32[8]{0:T(128)} %param.15) | copy-start | bytes 100
  6.5 203.1 %all-gather.4.cloned.1.call-start = ((), (), s32[]{:S(2)}) async-start(), calls=%async_computation.1 | async-start | bytes 10117120 | tf_op jit(solution)/shard_map/all_gather | solution.py:13
  10.3 32.9 %all-to-all-start = ((bf16[8,1,10,4096]{3,2,1,0:T(8,128)(2,1)}), bf16[8,1,10,4096]{3,2,1,0:T(8,128)(2,1)S(1)}, u32[]{:S(2)}, u32[]{:S(2)}) async-start(bf16[8,1,10,4096]{3,2,1,0:T(8,128)(2,1)} %broadcast_in_dim.54), calls=%async_computation | async-start | bytes 2097152 | tf_op jit(solution)/shard_map/all_to_all | solution.py:23
  17.0 584.9 %all-gather.6.cloned.1.call-start = ((), (), s32[]{:S(2)}) async-start(), calls=%async_computation.2 | async-start | bytes 2949120 | tf_op jit(solution)/shard_map/all_gather | solution.py:44
  222.4 5.0 collective-permute-start
  228.1 13.0 %collective-permute-start = (bf16[80,1024]{1,0:T(8,128)(2,1)}, bf16[80,1024]{1,0:T(8,128)(2,1)S(1)}, u32[]{:S(2)}, u32[]{:S(2)}) collective-permute-start(bf16[80,1024]{1,0:T(8,128)(2,1)} %get-tuple-element.420), channel_id=1, source_target_pairs={{0,64},{64,128},{128,192},{192,256},{256,320},{320,384},{384,448},... | collective-permute-start | bytes 491528 | tf_op jit(solution)/shard_map/while/body/eval_jaxpr/ppermute | solution.py:40
  241.8 6.8 %collective-permute-start = (bf16[80,1024]{1,0:T(8,128)(2,1)}, bf16[80,1024]{1,0:T(8,128)(2,1)S(1)}, u32[]{:S(2)}, u32[]{:S(2)}) collective-permute-start(bf16[80,1024]{1,0:T(8,128)(2,1)} %get-tuple-element.420), channel_id=1, source_target_pairs={{0,64},{64,128},{128,192},{192,256},{256,320},{320,384},{384,448},... | collective-permute-start | bytes 491528 | tf_op jit(solution)/shard_map/while/body/eval_jaxpr/ppermute | solution.py:40
  249.3 6.8 %collective-permute-start = (bf16[80,1024]{1,0:T(8,128)(2,1)}, bf16[80,1024]{1,0:T(8,128)(2,1)S(1)}, u32[]{:S(2)}, u32[]{:S(2)}) collective-permute-start(bf16[80,1024]{1,0:T(8,128)(2,1)} %get-tuple-element.420), channel_id=1, source_target_pairs={{0,64},{64,128},{128,192},{192,256},{256,320},{320,384},{384,448},... | collective-permute-start | bytes 491528 | tf_op jit(solution)/shard_map/while/body/eval_jaxpr/ppermute | solution.py:40
  256.8 6.8 %collective-permute-start = (bf16[80,1024]{1,0:T(8,128)(2,1)}, bf16[80,1024]{1,0:T(8,128)(2,1)S(1)}, u32[]{:S(2)}, u32[]{:S(2)}) collective-permute-start(bf16[80,1024]{1,0:T(8,128)(2,1)} %get-tuple-element.420), channel_id=1, source_target_pairs={{0,64},{64,128},{128,192},{192,256},{256,320},{320,384},{384,448},... | collective-permute-start | bytes 491528 | tf_op jit(solution)/shard_map/while/body/eval_jaxpr/ppermute | solution.py:40
  264.3 6.8 %collective-permute-start = (bf16[80,1024]{1,0:T(8,128)(2,1)}, bf16[80,1024]{1,0:T(8,128)(2,1)S(1)}, u32[]{:S(2)}, u32[]{:S(2)}) collective-permute-start(bf16[80,1024]{1,0:T(8,128)(2,1)} %get-tuple-element.420), channel_id=1, source_target_pairs={{0,64},{64,128},{128,192},{192,256},{256,320},{320,384},{384,448},... | collective-permute-start | bytes 491528 | tf_op jit(solution)/shard_map/while/body/eval_jaxpr/ppermute | solution.py:40
  271.9 92.8 %collective-permute-start = (bf16[80,1024]{1,0:T(8,128)(2,1)}, bf16[80,1024]{1,0:T(8,128)(2,1)S(1)}, u32[]{:S(2)}, u32[]{:S(2)}) collective-permute-start(bf16[80,1024]{1,0:T(8,128)(2,1)} %get-tuple-element.420), channel_id=1, source_target_pairs={{0,64},{64,128},{128,192},{192,256},{256,320},{320,384},{384,448},... | collective-permute-start | bytes 491528 | tf_op jit(solution)/shard_map/while/body/eval_jaxpr/ppermute | solution.py:40
  381.1 6.8 %collective-permute-start = (bf16[80,1024]{1,0:T(8,128)(2,1)}, bf16[80,1024]{1,0:T(8,128)(2,1)S(1)}, u32[]{:S(2)}, u32[]{:S(2)}) collective-permute-start(bf16[80,1024]{1,0:T(8,128)(2,1)} %get-tuple-element.420), channel_id=1, source_target_pairs={{0,64},{64,128},{128,192},{192,256},{256,320},{320,384},{384,448},... | collective-permute-start | bytes 491528 | tf_op jit(solution)/shard_map/while/body/eval_jaxpr/ppermute | solution.py:40
  404.3 6.8 %collective-permute-start = (bf16[80,1024]{1,0:T(8,128)(2,1)}, bf16[80,1024]{1,0:T(8,128)(2,1)S(1)}, u32[]{:S(2)}, u32[]{:S(2)}) collective-permute-start(bf16[80,1024]{1,0:T(8,128)(2,1)} %get-tuple-element.420), channel_id=1, source_target_pairs={{0,64},{64,128},{128,192},{192,256},{256,320},{320,384},{384,448},... | collective-permute-start | bytes 491528 | tf_op jit(solution)/shard_map/while/body/eval_jaxpr/ppermute | solution.py:40
  427.5 6.8 %collective-permute-start = (bf16[80,1024]{1,0:T(8,128)(2,1)}, bf16[80,1024]{1,0:T(8,128)(2,1)S(1)}, u32[]{:S(2)}, u32[]{:S(2)}) collective-permute-start(bf16[80,1024]{1,0:T(8,128)(2,1)} %get-tuple-element.420), channel_id=1, source_target_pairs={{0,64},{64,128},{128,192},{192,256},{256,320},{320,384},{384,448},... | collective-permute-start | bytes 491528 | tf_op jit(solution)/shard_map/while/body/eval_jaxpr/ppermute | solution.py:40
  450.7 6.8 %collective-permute-start = (bf16[80,1024]{1,0:T(8,128)(2,1)}, bf16[80,1024]{1,0:T(8,128)(2,1)S(1)}, u32[]{:S(2)}, u32[]{:S(2)}) collective-permute-start(bf16[80,1024]{1,0:T(8,128)(2,1)} %get-tuple-element.420), channel_id=1, source_target_pairs={{0,64},{64,128},{128,192},{192,256},{256,320},{320,384},{384,448},... | collective-permute-start | bytes 491528 | tf_op jit(solution)/shard_map/while/body/eval_jaxpr/ppermute | solution.py:40
  474.0 6.8 %collective-permute-start = (bf16[80,1024]{1,0:T(8,128)(2,1)}, bf16[80,1024]{1,0:T(8,128)(2,1)S(1)}, u32[]{:S(2)}, u32[]{:S(2)}) collective-permute-start(bf16[80,1024]{1,0:T(8,128)(2,1)} %get-tuple-element.420), channel_id=1, source_target_pairs={{0,64},{64,128},{128,192},{192,256},{256,320},{320,384},{384,448},... | collective-permute-start | bytes 491528 | tf_op jit(solution)/shard_map/while/body/eval_jaxpr/ppermute | solution.py:40
  497.2 6.8 %collective-permute-start = (bf16[80,1024]{1,0:T(8,128)(2,1)}, bf16[80,1024]{1,0:T(8,128)(2,1)S(1)}, u32[]{:S(2)}, u32[]{:S(2)}) collective-permute-start(bf16[80,1024]{1,0:T(8,128)(2,1)} %get-tuple-element.420), channel_id=1, source_target_pairs={{0,64},{64,128},{128,192},{192,256},{256,320},{320,384},{384,448},... | collective-permute-start | bytes 491528 | tf_op jit(solution)/shard_map/while/body/eval_jaxpr/ppermute | solution.py:40
  520.4 6.8 %collective-permute-start = (bf16[80,1024]{1,0:T(8,128)(2,1)}, bf16[80,1024]{1,0:T(8,128)(2,1)S(1)}, u32[]{:S(2)}, u32[]{:S(2)}) collective-permute-start(bf16[80,1024]{1,0:T(8,128)(2,1)} %get-tuple-element.420), channel_id=1, source_target_pairs={{0,64},{64,128},{128,192},{192,256},{256,320},{320,384},{384,448},... | collective-permute-start | bytes 491528 | tf_op jit(solution)/shard_map/while/body/eval_jaxpr/ppermute | solution.py:40
  543.6 3.9 collective-permute-start
Sparse Core Ops, SparseCore 0:
  11.8 197.7 all-gather.3
  552.0 49.8 all-gather.5
where the time goes:
time: 613 us; the launch traced here: 610 us
  waiting for transfers between devices  378 us (62%)
  matrix products  91.7 us (15%)
  local copies, waits for them, and re-layouts  68.9 us (11%)
  other arithmetic  31.1 us (5%)
  starting transfers between devices  25.9 us (4%)
  between operations  13.5 us (2%)
    all_gather x1, waiting for transfers between devices, gather_turned(): lax.all_gather(both, axis, axis=0, tiled=True)  166 us
    ppermute x15, waiting for transfers between devices, from_behind(): return lax.ppermute(block, axis, route)  138 us
    all_gather x1, waiting for transfers between devices, broadcast(): lax.all_gather(shard, axis)  50 us
    dot_general x8, matrix products, attend_layer(): jnp.dot(normed, qkv_weight, preferred_element_type=jnp.float32)  33.3 us
    all_to_all x1, waiting for transfers between devices, copy_for_each(): return lax.all_to_all(copies, axis, split_axis=0, concat_axis=0, tiled=True)  24.2 us
    reshape x24, local copies, waits for them, and re-layouts, split_heads(): return block.reshape(patch_count, PATCH, HEADS, head_dim)  20.8 us
    dot_general x8, matrix products, attend_layer(): jnp.einsum('phqk,pkhd->pqhd', weights, value_rows, preferred_element_type...  20.1 us
    ppermute x15, starting transfers between devices, from_behind(): return lax.ppermute(block, axis, route)  19.2 us
  transfers between devices with their start and end apart: 18, of which 17 were waited for; matrix products, arithmetic and copies ran while one was open for 6% of the time, Pallas kernels for 0%

commit v1 on v0

--- a/solution.py
+++ b/solution.py
@@ -10,7 +10,11 @@
 def gather_turned(arrays, axis, dims):
     turned = [jnp.moveaxis(a, dim, 0) for a, dim in zip(arrays, dims)]
     both = jnp.concatenate([t.reshape(len(t), -1) for t in turned], axis=1)
-    filled, at, gathered = (lax.all_gather(both, axis, axis=0, tiled=True), 0, [])
+    filled, at, gathered = (
+        jnp.concatenate(lax.all_to_all(jnp.stack(lax.psum(1, axis) * [both]), axis, 0, 0), 0),
+        0,
+        [],
+    )
     for t, dim in zip(turned, dims):
         piece = filled[:, at : at + t[0].size].reshape(-1, *t.shape[1:])
         gathered.append(jnp.moveaxis(piece, 0, dim))

time: 613 us -> 728 us (1.19)
  waiting for transfers between devices: 378 us -> 471 us
  starting transfers between devices: 25.9 us -> 44.5 us
    all_to_all x0 -> x1, waiting for transfers between devices: none -> 264 us  [gather_turned(): lax.all_to_all(jnp.stack(lax.psum(1, axis) * [both]), axis, 0, 0)]
    all_gather x1 -> x0, waiting for transfers between devices: 166 us -> none  [gather_turned(): lax.all_gather(both, axis, axis=0, tiled=True)]
    all_to_all x0 -> x1, starting transfers between devices: none -> 18.6 us  [gather_turned(): lax.all_to_all(jnp.stack(lax.psum(1, axis) * [both]), axis, 0, 0)]
    ppermute x15, waiting for transfers between devices: 138 us -> 123 us  [from_behind(): return lax.ppermute(block, axis, route)]
    all_gather x1, waiting for transfers between devices: 50 us -> 60.6 us  [broadcast(): lax.all_gather(shard, axis)]
  transfers between devices with their start and end apart: 18 -> 18, of which waited for: 17 -> 17; matrix products, arithmetic and copies ran while one was open for 6% -> 5% of each run, Pallas kernels for 0% -> 0%
where the time goes in v1:
time: 728 us; the launch traced here: 725 us
  waiting for transfers between devices  471 us (65%)
  matrix products  92.3 us (13%)
  local copies, waits for them, and re-layouts  73.3 us (10%)
  starting transfers between devices  44.5 us (6%)
  other arithmetic  29.5 us (4%)
  between operations  13.6 us (2%)
    all_to_all x1, waiting for transfers between devices, gather_turned(): lax.all_to_all(jnp.stack(lax.psum(1, axis) * [both]), axis, 0, 0)  264 us
    ppermute x15, waiting for transfers between devices, from_behind(): return lax.ppermute(block, axis, route)  123 us
    all_gather x1, waiting for transfers between devices, broadcast(): lax.all_gather(shard, axis)  60.6 us
    dot_general x8, matrix products, attend_layer(): jnp.dot(normed, qkv_weight, preferred_element_type=jnp.float32)  33.3 us
    all_to_all x1, waiting for transfers between devices, copy_for_each(): return lax.all_to_all(copies, axis, split_axis=0, concat_axis=0, tiled=True)  23.9 us
    reshape x24, local copies, waits for them, and re-layouts, split_heads(): return block.reshape(patch_count, PATCH, HEADS, head_dim)  20.8 us
    dot_general x8, matrix products, attend_layer(): jnp.einsum('phqk,pkhd->pqhd', weights, value_rows, preferred_element_type...  20.6 us
    ppermute x15, starting transfers between devices, from_behind(): return lax.ppermute(block, axis, route)  19.2 us
  transfers between devices with their start and end apart: 18, of which 17 were waited for; matrix products, arithmetic and copies ran while one was open for 5% of the time, Pallas kernels for 0%

profile of v1, /device:TPU:57, one launch (start us, length us, event | category | flops | bytes accessed | tf_op | source)
XLA Modules:
  0.0 725.2 jit_solution(10508697882519969304)
XLA Ops:
  6.5 2.0 broadcast_in_dim.54
  8.6 6.7 all-to-all-start.1
  15.3 23.9 %all-to-all-done.1 = bf16[8,1,10,4096]{3,2,1,0:T(8,128)(2,1)S(1)} async-done(((bf16[8,1,10,4096]{3,2,1,0:T(8,128)(2,1)}), bf16[8,1,10,4096]{3,2,1,0:T(8,128)(2,1)S(1)}, u32[]{:S(2)}, u32[]{:S(2)}) %all-to-all-start.1) | async-done | bytes 655392 | tf_op jit(solution)/shard_map/all_to_all | solution.py:27
  39.2 4.4 stack.2
  43.6 18.6 %all-to-all-start = ((bf16[64,16,4864]{2,1,0:T(8,128)(2,1)}), bf16[64,16,4864]{2,1,0:T(8,128)(2,1)}, u32[]{:S(2)}, u32[]{:S(2)}) async-start(bf16[64,16,4864]{2,1,0:T(8,128)(2,1)} %stack.2), calls=%async_computation | async-start | bytes 19922944 | tf_op jit(solution)/shard_map/all_to_all | solution.py:14
  64.7 264.2 %all-to-all-done = bf16[64,16,4864]{2,1,0:T(8,128)(2,1)} async-done(((bf16[64,16,4864]{2,1,0:T(8,128)(2,1)}), bf16[64,16,4864]{2,1,0:T(8,128)(2,1)}, u32[]{:S(2)}, u32[]{:S(2)}) %all-to-all-start) | async-done | bytes 9961504 | tf_op jit(solution)/shard_map/all_to_all | solution.py:14
  328.9 5.9 slice.42
  334.8 1.8 slice.43
  336.5 3.2 convolution_convert_fusion.2
  341.0 310.8 %while.16 = (s32[]{:T(128)}, bf16[80,1024]{1,0:T(8,128)(2,1)S(1)}, bf16[8,80,1024]{2,1,0:T(8,128)(2,1)}, s32[]{:T(128)}, pred[]{:T(512)}, /*index=5*/bf16[8,80,1...) while((s32[]{:T(128)}, bf16[80,1024]{1,0:T(8,128)(2,1)S(1)}, ...), condition=%wide.region_6.7_spmd, body=%wide.region_0.6_spmd.sunk | while | flops 676917632 | bytes 15702796 | solution.py:152
  349.2 3.9 collective-permute-done
  356.8 3.9 collective-permute-done
  364.3 3.9 collective-permute-done
  371.8 3.9 collective-permute-done
  379.3 3.9 collective-permute-done
  386.8 81.5 %collective-permute-done = bf16[80,1024]{1,0:T(8,128)(2,1)S(1)} collective-permute-done((bf16[80,1024]{1,0:T(8,128)(2,1)}, bf16[80,1024]{1,0:T(8,128)(2,1)S(1)}, u32[]{:S(2)}, u32[]{:S(2)}) %collective-permute-start) | collective-permute-done | bytes 163872 | tf_op jit(solution)/shard_map/while/body/eval_jaxpr/ppermute | solution.py:44
  468.3 16.5 %conditional.2 = (bf16[80,1024]{1,0:T(8,128)(2,1)}) conditional(s32[]{:T(128)} %convert_element_type.127, () %tuple.47, (pred[]{:T(512)}, bf16[8,80,1024]{2,1,0:T(8,128)(2,1)}, s32[]{:T(128)}, bf16[80,1024]{1,0:T(8,128)(2,1)S(1)}, bf16[8,80,1024]{2,1,0:T(8,128)(2,1)}, /*index=5*/bf16[1024]{0:T(1024)(128)(2,1)S(1)}, bf16[1024,3072]{1,0:T(8,128)(2,1)}, ...), branch_computations={%region_1.1_spmd, %region_2.5_spmd} | conditional | flops 676835712 | bytes 14227409 | solution.py:135
  469.5 4.2 convolution_convert_fusion
  478.9 2.6 fusion.4
  482.7 2.1 fusion.5
  487.0 1.6 bitcast_dynamic-update-slice_fusion.2
  488.6 3.0 collective-permute-done
  491.6 16.5 %conditional.2 = (bf16[80,1024]{1,0:T(8,128)(2,1)}) conditional(s32[]{:T(128)} %convert_element_type.127, () %tuple.47, (pred[]{:T(512)}, bf16[8,80,1024]{2,1,0:T(8,128)(2,1)}, s32[]{:T(128)}, bf16[80,1024]{1,0:T(8,128)(2,1)S(1)}, bf16[8,80,1024]{2,1,0:T(8,128)(2,1)}, /*index=5*/bf16[1024]{0:T(1024)(128)(2,1)S(1)}, bf16[1024,3072]{1,0:T(8,128)(2,1)}, ...), branch_computations={%region_1.1_spmd, %region_2.5_spmd} | conditional | flops 676835712 | bytes 14227409 | solution.py:135
  492.8 4.2 convolution_convert_fusion
  502.2 2.6 fusion.4
  506.0 2.1 fusion.5
  510.3 1.6 bitcast_dynamic-update-slice_fusion.2
  511.9 3.0 collective-permute-done
  514.9 16.5 %conditional.2 = (bf16[80,1024]{1,0:T(8,128)(2,1)}) conditional(s32[]{:T(128)} %convert_element_type.127, () %tuple.47, (pred[]{:T(512)}, bf16[8,80,1024]{2,1,0:T(8,128)(2,1)}, s32[]{:T(128)}, bf16[80,1024]{1,0:T(8,128)(2,1)S(1)}, bf16[8,80,1024]{2,1,0:T(8,128)(2,1)}, /*index=5*/bf16[1024]{0:T(1024)(128)(2,1)S(1)}, bf16[1024,3072]{1,0:T(8,128)(2,1)}, ...), branch_computations={%region_1.1_spmd, %region_2.5_spmd} | conditional | flops 676835712 | bytes 14227409 | solution.py:135
  516.1 4.2 convolution_convert_fusion
  525.5 2.6 fusion.4
  529.3 2.1 fusion.5
  533.6 1.6 bitcast_dynamic-update-slice_fusion.2
  535.2 3.0 collective-permute-done
  538.2 16.5 %conditional.2 = (bf16[80,1024]{1,0:T(8,128)(2,1)}) conditional(s32[]{:T(128)} %convert_element_type.127, () %tuple.47, (pred[]{:T(512)}, bf16[8,80,1024]{2,1,0:T(8,128)(2,1)}, s32[]{:T(128)}, bf16[80,1024]{1,0:T(8,128)(2,1)S(1)}, bf16[8,80,1024]{2,1,0:T(8,128)(2,1)}, /*index=5*/bf16[1024]{0:T(1024)(128)(2,1)S(1)}, bf16[1024,3072]{1,0:T(8,128)(2,1)}, ...), branch_computations={%region_1.1_spmd, %region_2.5_spmd} | conditional | flops 676835712 | bytes 14227409 | solution.py:135
  539.4 4.2 convolution_convert_fusion
  548.8 2.6 fusion.4
  552.6 2.1 fusion.5
  556.9 1.7 bitcast_dynamic-update-slice_fusion.2
  558.6 2.9 collective-permute-done
  561.5 16.5 %conditional.2 = (bf16[80,1024]{1,0:T(8,128)(2,1)}) conditional(s32[]{:T(128)} %convert_element_type.127, () %tuple.47, (pred[]{:T(512)}, bf16[8,80,1024]{2,1,0:T(8,128)(2,1)}, s32[]{:T(128)}, bf16[80,1024]{1,0:T(8,128)(2,1)S(1)}, bf16[8,80,1024]{2,1,0:T(8,128)(2,1)}, /*index=5*/bf16[1024]{0:T(1024)(128)(2,1)S(1)}, bf16[1024,3072]{1,0:T(8,128)(2,1)}, ...), branch_computations={%region_1.1_spmd, %region_2.5_spmd} | conditional | flops 676835712 | bytes 14227409 | solution.py:135
  562.7 4.2 convolution_convert_fusion
  572.1 2.6 fusion.4
  575.9 2.1 fusion.5
  581.8 3.0 collective-permute-done
  584.8 16.5 %conditional.2 = (bf16[80,1024]{1,0:T(8,128)(2,1)}) conditional(s32[]{:T(128)} %convert_element_type.127, () %tuple.47, (pred[]{:T(512)}, bf16[8,80,1024]{2,1,0:T(8,128)(2,1)}, s32[]{:T(128)}, bf16[80,1024]{1,0:T(8,128)(2,1)S(1)}, bf16[8,80,1024]{2,1,0:T(8,128)(2,1)}, /*index=5*/bf16[1024]{0:T(1024)(128)(2,1)S(1)}, bf16[1024,3072]{1,0:T(8,128)(2,1)}, ...), branch_computations={%region_1.1_spmd, %region_2.5_spmd} | conditional | flops 676835712 | bytes 14227409 | solution.py:135
  586.0 4.2 convolution_convert_fusion
  595.4 2.6 fusion.4
  599.2 2.1 fusion.5
  603.5 1.6 bitcast_dynamic-update-slice_fusion.2
  605.1 3.0 collective-permute-done
  608.1 16.5 %conditional.2 = (bf16[80,1024]{1,0:T(8,128)(2,1)}) conditional(s32[]{:T(128)} %convert_element_type.127, () %tuple.47, (pred[]{:T(512)}, bf16[8,80,1024]{2,1,0:T(8,128)(2,1)}, s32[]{:T(128)}, bf16[80,1024]{1,0:T(8,128)(2,1)S(1)}, bf16[8,80,1024]{2,1,0:T(8,128)(2,1)}, /*index=5*/bf16[1024]{0:T(1024)(128)(2,1)S(1)}, bf16[1024,3072]{1,0:T(8,128)(2,1)}, ...), branch_computations={%region_1.1_spmd, %region_2.5_spmd} | conditional | flops 676835712 | bytes 14227409 | solution.py:135
  609.3 4.2 convolution_convert_fusion
  618.7 2.6 fusion.4
  622.5 2.1 fusion.5
  626.8 1.6 bitcast_dynamic-update-slice_fusion.2
  628.4 3.0 collective-permute-done
  631.4 16.5 %conditional.2 = (bf16[80,1024]{1,0:T(8,128)(2,1)}) conditional(s32[]{:T(128)} %convert_element_type.127, () %tuple.47, (pred[]{:T(512)}, bf16[8,80,1024]{2,1,0:T(8,128)(2,1)}, s32[]{:T(128)}, bf16[80,1024]{1,0:T(8,128)(2,1)S(1)}, bf16[8,80,1024]{2,1,0:T(8,128)(2,1)}, /*index=5*/bf16[1024]{0:T(1024)(128)(2,1)S(1)}, bf16[1024,3072]{1,0:T(8,128)(2,1)}, ...), branch_computations={%region_1.1_spmd, %region_2.5_spmd} | conditional | flops 676835712 | bytes 14227409 | solution.py:135
  632.6 4.2 convolution_convert_fusion
  642.0 2.6 fusion.4
  645.8 2.1 fusion.5
  651.7 1.7 fusion.19
  653.4 2.7 fusion.29
  656.2 60.6 %all-gather.3.cloned.1.call-done = bf16[64,80,256]{2,1,0:T(8,128)(2,1)} async-done(((bf16[8,80,256]{2,1,0:T(8,128)(2,1)}), bf16[64,80,256]{2,1,0:T(8,128)(2,1)}) %all-gather.3.cloned.1.call-update) | async-done | bytes 2621456 | tf_op jit(solution)/shard_map/all_gather | solution.py:48
  (186 shorter events, 118.1 us)
Async XLA Ops:
  6.5 56.1 %copy-start = (bf16[256,1024]{1,0:T(8,128)(2,1)S(1)}, bf16[256,1024]{1,0:T(8,128)(2,1)}, u32[]{:S(2)}) copy-start(bf16[256,1024]{1,0:T(8,128)(2,1)} %param.17) | copy-start | bytes 1572868
  6.5 8.7 %copy-start.1 = (bf16[1,16,3072]{2,1,0:T(8,128)(2,1)S(1)}, bf16[1,16,3072]{2,1,0:T(8,128)(2,1)}, u32[]{:S(2)}) copy-start(bf16[1,16,3072]{2,1,0:T(8,128)(2,1)} %param.18) | copy-start | bytes 294916
  6.5 8.7 %copy-start.2 = (bf16[1,16,1024]{2,1,0:T(8,128)(2,1)S(1)}, bf16[1,16,1024]{2,1,0:T(8,128)(2,1)}, u32[]{:S(2)}) copy-start(bf16[1,16,1024]{2,1,0:T(8,128)(2,1)} %param.19) | copy-start | bytes 98308
  6.5 8.7 %copy-start.3 = (bf16[512,16]{0,1:T(8,128)(2,1)S(1)}, bf16[512,16]{0,1:T(8,128)(2,1)}, u32[]{:S(2)}) copy-start(bf16[512,16]{0,1:T(8,128)(2,1)} %param.21) | copy-start | bytes 49156
  6.5 8.8 %copy-start.4 = (bf16[256,16]{0,1:T(8,128)(2,1)S(1)}, bf16[256,16]{0,1:T(8,128)(2,1)}, u32[]{:S(2)}) copy-start(bf16[256,16]{0,1:T(8,128)(2,1)} %param.23) | copy-start | bytes 24580
  8.6 30.6 %all-to-all-start.1 = ((bf16[8,1,10,4096]{3,2,1,0:T(8,128)(2,1)}), bf16[8,1,10,4096]{3,2,1,0:T(8,128)(2,1)S(1)}, u32[]{:S(2)}, u32[]{:S(2)}) async-start(bf16[8,1,10,4096]{3,2,1,0:T(8,128)(2,1)} %broadcast_in_dim.54), calls=%async_computation.1 | async-start | bytes 2097152 | tf_op jit(solution)/shard_map/all_to_all | solution.py:27
  43.6 18.6 %copy-start.6 = (s32[8,80]{1,0:T(8,128)S(1)}, s32[8,80]{1,0:T(8,128)}, u32[]{:S(2)}) copy-start(s32[8,80]{1,0:T(8,128)} %param.14) | copy-start | bytes 7684
  43.6 18.9 %copy-start.7 = (bf16[1024]{0:T(1024)(128)(2,1)S(1)}, bf16[1024]{0:T(1024)(128)(2,1)}, u32[]{:S(2)}) copy-start(bf16[1024]{0:T(1024)(128)(2,1)} %param.22) | copy-start | bytes 6148
  43.6 18.9 %copy-start.5 = (bf16[1,1024]{1,0:T(2,128)(2,1)S(1)}, bf16[1,1024]{1,0:T(2,128)(2,1)}, u32[]{:S(2)}) copy-start(bf16[1,1024]{1,0:T(2,128)(2,1)} %param.20) | copy-start | bytes 6148
  43.6 19.0 %copy-start.8 = (s32[8]{0:T(128)S(1)}, s32[8]{0:T(128)}, u32[]{:S(2)}) copy-start(s32[8]{0:T(128)} %param.15) | copy-start | bytes 100
  43.6 285.3 %all-to-all-start = ((bf16[64,16,4864]{2,1,0:T(8,128)(2,1)}), bf16[64,16,4864]{2,1,0:T(8,128)(2,1)}, u32[]{:S(2)}, u32[]{:S(2)}) async-start(bf16[64,16,4864]{2,1,0:T(8,128)(2,1)} %stack.2), calls=%async_computation | async-start | bytes 19922944 | tf_op jit(solution)/shard_map/all_to_all | solution.py:14
  62.2 654.6 %all-gather.3.cloned.1.call-start = ((), (), s32[]{:S(2)}) async-start(), calls=%async_computation.2 | async-start | bytes 2949120 | tf_op jit(solution)/shard_map/all_gather | solution.py:48
  341.7 3.9 collective-permute-start
  346.3 6.8 collective-permute-start
  353.8 6.8 collective-permute-start
  361.3 6.8 collective-permute-start
  368.8 6.8 collective-permute-start
  376.4 6.8 collective-permute-start
  383.9 84.4 %collective-permute-start = (bf16[80,1024]{1,0:T(8,128)(2,1)}, bf16[80,1024]{1,0:T(8,128)(2,1)S(1)}, u32[]{:S(2)}, u32[]{:S(2)}) collective-permute-start(bf16[80,1024]{1,0:T(8,128)(2,1)} %get-tuple-element.420), channel_id=1, source_target_pairs={{0,64},{64,128},{128,192},{192,256},{256,320},{320,384},{384,448},... | collective-permute-start | bytes 491528 | tf_op jit(solution)/shard_map/while/body/eval_jaxpr/ppermute | solution.py:44
  484.8 6.8 collective-permute-start
  508.1 6.8 collective-permute-start
  531.4 6.8 collective-permute-start
  554.7 6.8 collective-permute-start
  578.0 6.8 collective-permute-start
  601.3 6.8 collective-permute-start
  624.6 6.8 collective-permute-start
  647.9 3.9 collective-permute-start
Sparse Core Ops, SparseCore 0:
  656.3 60.4 all-gather.2
